TPU v7x, 32 devices: a 4x4x1 block of a 4x4x8 slice. The times are simulated.
32 devices in a mesh: data: 1 (over z), hid: 4 (over y), vocab: 8 (over x, core).
Axes of the slice: x: 4, y: 4, z: 1, core: 2. Of those that a mesh axis runs over, the one named last changes fastest.
The devices are a block of a 4x4x8 slice.
Arguments:
- h_states: bfloat16 [1024, 6144], P('data', 'hid')
- w_head: bfloat16 [6144, 32768], P('hid', 'vocab')
- inv_temp: float32 [1024], P('data')
- tgt_ids: int32 [1024], P('data')
Outputs:
- output 1: float32 [1024, 32768], P('data', ('vocab', 'hid'))
- output 2: float32 [1024], P('data')
All inputs are finite; a program needn't handle non-finite values.
Results may differ from a plain program's by a relative error of at most 0.001.
Values are sent between devices in bfloat16 or wider.
A program may use at most 768 MiB of HBM per device.

v0:
```python
import jax
import jax.numpy as jnp
from jax import lax
from jax.sharding import PartitionSpec as P


def solution(mesh):
    hid_size = mesh.shape["hid"]
    voc_size = mesh.shape["vocab"]

    def local_step(h_blk, w_blk, temp_blk, tgt_blk):
        part_logits = jnp.dot(h_blk, w_blk, preferred_element_type=jnp.float32)
        logits = lax.psum_scatter(part_logits, "hid", scatter_dimension=1, tiled=True) * temp_blk[:, None]
        local_cols = logits.shape[1]
        glob_max = lax.pmax(jnp.max(logits, axis=1), ("vocab", "hid"))
        exp_vals = jnp.exp(logits - glob_max[:, None])
        glob_sum = lax.psum(jnp.sum(exp_vals, axis=1), ("vocab", "hid"))
        local_cdf = jnp.cumsum(exp_vals / glob_sum[:, None], axis=1)
        hid_tots = lax.all_gather(local_cdf[:, -1], "hid")
        vocab_tots = lax.all_gather(jnp.sum(hid_tots, axis=0), "vocab")
        hid_idx = lax.axis_index("hid")
        voc_idx = lax.axis_index("vocab")
        hid_off = jnp.sum(jnp.where((jnp.arange(hid_size) < hid_idx)[:, None], hid_tots, 0.0), axis=0)
        voc_off = jnp.sum(jnp.where((jnp.arange(voc_size) < voc_idx)[:, None], vocab_tots, 0.0), axis=0)
        cdf_blk = local_cdf + (voc_off + hid_off)[:, None]
        col_start = (voc_idx * hid_size + hid_idx) * local_cols
        local_pos = tgt_blk - col_start
        in_range = (local_pos >= 0) & (local_pos < local_cols)
        picked = jnp.take_along_axis(cdf_blk, jnp.clip(local_pos, 0, local_cols - 1)[:, None], axis=1)[:, 0]
        cdf_tgt = lax.psum(jnp.where(in_range, picked, 0.0), ("vocab", "hid"))
        return cdf_blk, cdf_tgt

    return jax.shard_map(local_step, mesh=mesh, in_specs=(P("data", "hid"), P("hid", "vocab"), P("data"), P("data")), out_specs=(P("data", ("vocab", "hid")), P("data")), check_vma=False)
```

profile of v0, /device:TPU:97, one launch (start us, length us, event | category | flops | bytes accessed | tf_op | source)
XLA Modules:
  0.0 408.2 jit_solution(8215045858289389451)
XLA Ops:
  7.2 0.0 copy-start
  7.2 0.1 reduce-scatter.2.cloned.1.call-start
  7.3 1.8 copy-done
  9.1 19.3 %fusion.5 = f32[1024,4096]{1,0:T(8,128)} fusion(bf16[1024,1536]{1,0:T(8,128)(2,1)S(1)} %copy-done, bf16[1536,4096]{1,0:T(8,128)(2,1)} %param.5), kind=kOutput, calls=%fused_computation.21 | convolution fusion | flops 12884901888 | bytes 32505856 | tf_op jit(solution)/shard_map/dot_general | solution.py:12
  28.4 0.1 reduce-scatter.2.cloned.1.call-update
  28.5 0.6 copy-done.5
  29.1 148.6 %reduce-scatter.2.cloned.1.call-done = f32[1024,1024]{1,0:T(8,128)} async-done(((f32[1024,4096]{1,0:T(8,128)}), f32[1024,1024]{1,0:T(8,128)}) %reduce-scatter.2.cloned.1.call-update) | async-done | bytes 4194320 | tf_op jit(solution)/shard_map/reduce_scatter | solution.py:13
  177.7 2.7 multiply_reduce_fusion
  180.4 45.2 %pmax.7 = f32[1024]{0:T(1024)S(1)} all-reduce(f32[1024]{0:T(1024)S(1)} %multiply_reduce_fusion), channel_id=1, replica_groups=mesh['data'=1,'hid'=4,'vocab'=8] {'vocab','hid'}, use_global_device_ids=true, to_apply=%region_2.0 | all-reduce | flops 1024 | bytes 8192 | tf_op jit(solution)/shard_map/pmax | solution.py:15
  225.6 3.1 fusion
  228.7 44.4 %psum.14 = f32[1024]{0:T(1024)S(1)} all-reduce(f32[1024]{0:T(1024)S(1)} %fusion), channel_id=1, replica_groups=mesh['data'=1,'hid'=4,'vocab'=8] {'vocab','hid'}, use_global_device_ids=true, to_apply=%region_4.0 | all-reduce | flops 1024 | bytes 8192 | tf_op jit(solution)/shard_map/psum | solution.py:17
  273.1 2.7 divide_bitcast_fusion
  275.8 3.0 copy.16
  278.9 5.4 %copy.13 = f32[1024,8,128]{0,1,2:T(8,128)} copy(f32[1024,8,128]{2,1,0:T(8,128)} %bitcast.17) | data formatting | bytes 8388608 | tf_op jit(solution)/shard_map/reshape.2
  284.3 2.5 fusion.4
  286.8 0.0 copy-start.2
  286.8 2.0 copy-done.2
  288.9 2.6 broadcast_add_fusion.1
  291.5 2.4 copy.14
  294.0 0.0 copy-start.3
  294.0 2.0 copy-done.3
  296.0 5.4 %copy.15 = f32[1024,1024]{1,0:T(8,128)} copy(f32[1024,1024]{0,1:T(8,128)} %bitcast.16) | data formatting | bytes 8388608 | tf_op jit(solution)/shard_map/reduce_window_sum
  301.3 8.9 %all-gather = f32[4096,1]{0,1:T(1,128)S(1)} all-gather(f32[1024,1]{0,1:T(1,128)S(1)} %slice.16), channel_id=2, replica_groups=mesh['data'=1,'hid'=4,'vocab'=8] {'hid'}, dimensions={0}, use_global_device_ids=true | all-gather | bytes 20480 | tf_op jit(solution)/shard_map/all_gather | solution.py:19
  310.3 0.5 broadcast.51
  310.8 0.7 reduce.3
  311.5 0.1 select_reduce_fusion.1
  311.6 19.8 %all-gather.1 = f32[8192]{0:T(1024)S(1)} all-gather(f32[1024]{0:T(1024)S(1)} %get-tuple-element.3), channel_id=3, replica_groups=mesh['data'=1,'hid'=4,'vocab'=8] {'vocab'}, dimensions={0}, use_global_device_ids=true | all-gather | bytes 36864 | tf_op jit(solution)/shard_map/all_gather | solution.py:20
  331.4 0.1 select_reduce_fusion
  331.5 0.0 copy-start.1
  331.5 4.7 %broadcast_add_fusion = f32[1024,1024]{1,0:T(8,128)} fusion(f32[1024,1024]{1,0:T(8,128)} %copy.15, f32[1024]{0:T(1024)S(1)} %add.31), kind=kLoop, calls=%fused_computation.5 | loop fusion | flops 1048576 | bytes 8392704 | tf_op jit(solution)/shard_map/add | solution.py:25
  336.2 16.8 %gather_fusion = f32[1024]{0:T(1024)S(1)} fusion(f32[1024,1024]{1,0:T(8,128)} %broadcast_add_fusion, s32[1024]{0:T(1024)S(1)} %bitcast.14), kind=kCustom, calls=%fused_computation | custom fusion | bytes 16384 | tf_op jit(solution)/shard_map/jit(take_along_axis)/gather | solution.py:29
  353.1 48.3 %psum.15 = f32[1024]{0:T(1024)} all-reduce(f32[1024]{0:T(1024)S(1)} %select_select_fusion), channel_id=1, replica_groups=mesh['data'=1,'hid'=4,'vocab'=8] {'vocab','hid'}, use_global_device_ids=true, to_apply=%region_10.11 | all-reduce | flops 1024 | bytes 8192 | tf_op jit(solution)/shard_map/psum | solution.py:30
  (18 shorter events, 0.2 us)
Async XLA Ops:
  7.2 1.9 copy-start
  7.2 170.5 %reduce-scatter.2.cloned.1.call-start = ((), (), s32[]{:S(2)}) async-start(), calls=%async_computation.1 | async-start | bytes 20971520 | tf_op jit(solution)/shard_map/reduce_scatter | solution.py:13
  28.4 0.7 copy-start.5
  28.4 149.3 %copy-start.4 = (f32[1024]{0:T(1024)S(1)}, f32[1024]{0:T(1024)}, u32[]{:S(2)}) copy-start(f32[1024]{0:T(1024)} %param.6) | copy-start | bytes 12292
  286.8 2.0 copy-start.2
  294.0 2.0 copy-start.3
  331.5 69.9 %copy-start.1 = (bf16[1024,1536]{1,0:T(8,128)(2,1)S(1)}, bf16[1024,1536]{1,0:T(8,128)(2,1)}, u32[]{:S(2)}) copy-start(bf16[1024,1536]{1,0:T(8,128)(2,1)} %param.4) | copy-start | bytes 9437188
Sparse Core Ops, SparseCore 0:
  28.6 149.1 reduce-scatter.1
where the time goes:
time: 409 us; the launch traced here: 408 us
  blocking collectives  167 us (41%)
  waiting for transfers between devices  149 us (36%)
  local copies, waits for them, and re-layouts  40.1 us (10%)
  matrix products  19.3 us (5%)
  other arithmetic  19.3 us (5%)
  between operations  14.2 us (3%)
    reduce_scatter x1, waiting for transfers between devices, local_step(): lax.psum_scatter(part_logits, 'hid', scatter_dimension=1, tiled=True)  149 us
    psum x1, blocking collectives, local_step(): cdf_tgt = lax.psum(jnp.where(in_range, picked, 0.0), ('vocab', 'hid'))  48.3 us
    pmax x1, blocking collectives, local_step(): glob_max = lax.pmax(jnp.max(logits, axis=1), ('vocab', 'hid'))  45.2 us
    psum x1, blocking collectives, local_step(): glob_sum = lax.psum(jnp.sum(exp_vals, axis=1), ('vocab', 'hid'))  44.4 us
    all_gather x1, blocking collectives, local_step(): vocab_tots = lax.all_gather(jnp.sum(hid_tots, axis=0), 'vocab')  19.8 us
    dot_general x1, matrix products, local_step(): part_logits = jnp.dot(h_blk, w_blk, preferred_element_type=jnp.float32)  19.3 us
    gather x1, local copies, waits for them, and re-layouts, local_step(): jnp.take_along_axis(cdf_blk, jnp.clip(local_pos, 0, local_cols - 1)[:, No...  16.8 us
    another operation x5, local copies, waits for them, and re-layouts  13.2 us
  transfers between devices with their start and end apart: 1, of which 1 were waited for; matrix products, arithmetic and copies ran while one was open for 0% of the time, Pallas kernels for 0%

commit v1 on v0

v1 whole, which is shorter than its diff:
```python
import functools

import jax
import jax.numpy as jnp
from jax import lax
from jax.experimental import pallas as pl
from jax.experimental.pallas import tpu as pltpu
from jax.sharding import PartitionSpec as P

MESH = pl.DeviceIdType.MESH
R = 128
LANES = 128
TRI = 256


def head_kernel(nh, nv, h_hbm, w_hbm, temp_ref, tgt_ref,
                c_hbm, scale_ref, off_ref, ctgt_ref,
                h_own, h_nb, w_sum, w_own, w_leaf, w_dir, s_send, s_recv, z_buf,
                stat_y, stat_x,
                ld_sem, hy_ss, hy_rs, hx_ss, hx_rs, leaf_ss, leaf_rs, dir_ss, dir_rs,
                sum_ss, sum_rs, sty_ss, sty_rs, stx_ss, stx_rs, out_sem):
    rows, depth = h_hbm.shape
    cb = w_hbm.shape[1] // nh
    hc = cb // 2
    nr = rows // R
    piece = rows // nv
    half = piece // 2

    me = lax.axis_index("hid")
    vi = lax.axis_index("vocab")
    up = lax.rem(me + 1, nh)
    dn = lax.rem(me + nh - 1, nh)
    far = lax.rem(me + 2, nh)
    nxt = lax.rem(vi + 2, nv)
    prv = lax.rem(vi + nv - 2, nv)
    opp = lax.rem(vi + 4, nv)
    mate = vi + 1 - 2 * lax.rem(vi, 2)

    def tok(d, part):
        return pl.ds(pl.multiple_of(d * cb + part * hc, LANES), hc)

    def rws(start, n):
        return pl.ds(pl.multiple_of(start, n), n)

    def rdma(src, dst, ss, rs, dev):
        return pltpu.make_async_remote_copy(
            src_ref=src, dst_ref=dst, send_sem=ss, recv_sem=rs,
            device_id=dev, device_id_type=MESH)

    loads = [
        pltpu.make_async_copy(h_hbm, h_own, ld_sem.at[0]),
        pltpu.make_async_copy(w_hbm.at[:, tok(dn, 0)], w_sum.at[0], ld_sem.at[1]),
        pltpu.make_async_copy(w_hbm.at[:, tok(up, 1)], w_sum.at[1], ld_sem.at[2]),
        pltpu.make_async_copy(
            w_hbm.at[:, pl.ds(pl.multiple_of(me * cb, LANES), cb)], w_own, ld_sem.at[3]),
    ]
    for c in loads:
        c.start()

    barrier = pltpu.get_barrier_semaphore()
    for j in range(1, nh):
        pl.semaphore_signal(barrier, inc=1, device_id={"hid": lax.rem(me + j, nh)},
                            device_id_type=MESH)
    for j in range(1, nv):
        pl.semaphore_signal(barrier, inc=1, device_id={"vocab": lax.rem(vi + j, nv)},
                            device_id_type=MESH)
    pl.semaphore_wait(barrier, nh - 1 + nv - 1)

    to_dn, to_up = {"hid": dn}, {"hid": up}
    mine = rws(vi * piece, piece)
    hy = [rdma(h_hbm.at[mine], h_nb.at[0, mine], hy_ss.at[0], hy_rs.at[0], to_dn),
          rdma(h_hbm.at[mine], h_nb.at[1, mine], hy_ss.at[1], hy_rs.at[1], to_up)]
    leaf = [rdma(w_hbm.at[:, tok(far, 0)], w_leaf.at[0], leaf_ss.at[0], leaf_rs.at[0], to_dn),
            rdma(w_hbm.at[:, tok(far, 1)], w_leaf.at[1], leaf_ss.at[1], leaf_rs.at[1], to_up)]
    direct = [rdma(w_hbm.at[:, tok(up, 0)], w_dir.at[0], dir_ss.at[0], dir_rs.at[0], to_up),
              rdma(w_hbm.at[:, tok(dn, 1)], w_dir.at[1], dir_ss.at[1], dir_rs.at[1], to_dn)]
    for c in hy + leaf:
        c.start()

    to_nxt, to_prv, to_mate = {"vocab": nxt}, {"vocab": prv}, {"vocab": mate}

    def hx(a, k, at, dev):
        return rdma(h_nb.at[a, at], h_nb.at[a, at], hx_ss.at[a, k], hx_rs.at[a, k], dev)

    from_prv = rws(prv * piece, piece)
    from_nxt = rws(nxt * piece, piece)
    opp_all = rws(opp * piece, piece)
    started = []

    def go(c):
        c.start()
        started.append(c)

    for a in range(2):
        hy[a].wait_recv()
        go(hx(a, 0, mine, to_nxt))
        go(hx(a, 1, mine, to_prv))
        go(hx(a, 4, mine, to_mate))
    for c in direct:
        c.start()

    for c in loads:
        c.wait()

    def own(i, _):
        at = rws(i * R, R)
        x = h_own[at]
        for p in range(2):
            s_send[p, at] = jnp.dot(x, w_sum[p], preferred_element_type=jnp.float32)
        for p in range(2):
            z_buf[at, p * hc:(p + 1) * hc] = jnp.dot(
                x, w_own[:, p * hc:(p + 1) * hc], preferred_element_type=jnp.float32)
        return 0

    lax.fori_loop(0, nr, own, 0)

    for a in range(2):
        hx(a, 0, from_prv, to_nxt).wait_recv()
        lo = rws(prv * piece, half)
        go(hx(a, 2, lo, to_nxt))
        go(hx(a, 5, from_prv, to_mate))
        hx(a, 1, from_nxt, to_prv).wait_recv()
        hi = rws(nxt * piece + half, half)
        go(hx(a, 3, hi, to_prv))
        go(hx(a, 6, from_nxt, to_mate))
    for a in range(2):
        hx(a, 2, rws(opp * piece, half), to_nxt).wait_recv()
        hx(a, 3, rws(opp * piece + half, half), to_prv).wait_recv()
        go(hx(a, 7, opp_all, to_mate))
    for a in range(2):
        for k in range(4, 8):
            hx(a, k, mine, to_mate).wait_recv()

    for c in leaf:
        c.wait_recv()

    def sum_copy(p, i):
        at = rws(i * R, R)
        return rdma(s_send.at[p, at], s_recv.at[p, at], sum_ss.at[p, i], sum_rs.at[p, i],
                    to_dn if p == 0 else to_up)

    def add_leaf(i, _):
        at = rws(i * R, R)
        for p in range(2):
            s_send[p, at] = s_send[p, at] + jnp.dot(
                h_nb[p, at], w_leaf[p], preferred_element_type=jnp.float32)
        for p in range(2):
            sum_copy(p, i).start()
        return 0

    lax.fori_loop(0, nr, add_leaf, 0)

    for c in direct:
        c.wait_recv()

    tri = (lax.broadcasted_iota(jnp.int32, (TRI, TRI), 0)
           <= lax.broadcasted_iota(jnp.int32, (TRI, TRI), 1)).astype(jnp.bfloat16)
    col = lax.broadcasted_iota(jnp.int32, (R, TRI), 1).astype(jnp.float32)
    lane = lax.broadcasted_iota(jnp.int32, (R, LANES), 1)
    first_tok = ((vi * nh + me) * cb).astype(jnp.float32)

    def out_copy(i):
        at = rws(i * R, R)
        return pltpu.make_async_copy(z_buf.at[at], c_hbm.at[at], out_sem.at[i])

    def by_row(v):
        return jnp.broadcast_to(v, (LANES, R)).T

    def softmax(i, _):
        at = rws(i * R, R)
        for p in range(2):
            sl = slice(p * hc, (p + 1) * hc)
            z_buf[at, sl] = z_buf[at, sl] + jnp.dot(
                h_nb[1 - p, at], w_dir[p], preferred_element_type=jnp.float32)
        temp = jnp.concatenate([by_row(temp_ref[pl.ds(i, 1)])] * (TRI // LANES), axis=1)
        tgt = jnp.concatenate(
            [by_row(tgt_ref[pl.ds(i, 1)].astype(jnp.float32) - first_tok)] * (TRI // LANES), axis=1)
        for p in range(2):
            sum_copy(p, i).wait_recv()
        m = None
        zs = []
        for b in range(cb // TRI):
            p, o = divmod(b * TRI, hc)
            z = (z_buf[at, b * TRI:(b + 1) * TRI] + s_recv[p, at, o:o + TRI]) * temp
            zs.append(z)
            m = z if m is None else jnp.maximum(m, z)
        m = jnp.max(m, axis=1, keepdims=True)
        carry = jnp.zeros((R, 1), jnp.float32)
        picked = jnp.zeros((R, TRI), jnp.float32)
        for b in range(cb // TRI):
            e = jnp.exp(zs[b] - m)
            picked = picked + jnp.where(col + float(b * TRI) <= tgt, e, 0.0)
            e1 = e.astype(jnp.bfloat16)
            r1 = e - e1.astype(jnp.float32)
            e2 = r1.astype(jnp.bfloat16)
            e3 = (r1 - e2.astype(jnp.float32)).astype(jnp.bfloat16)
            c = (jnp.dot(e3, tri, preferred_element_type=jnp.float32)
                 + jnp.dot(e2, tri, preferred_element_type=jnp.float32)
                 + jnp.dot(e1, tri, preferred_element_type=jnp.float32)) + carry
            z_buf[at, b * TRI:(b + 1) * TRI] = c
            carry = c[:, TRI - 1:TRI]
        out_copy(i).start()
        t = jnp.sum(picked, axis=1, keepdims=True)
        st = jnp.where(lane == 0, m, jnp.where(lane == 1, carry, jnp.where(lane == 2, t, 0.0))).T
        for k in range(3):
            stat_y[me, k, pl.ds(i, 1)] = st[k:k + 1]
        return 0

    lax.fori_loop(0, nr, softmax, 0)

    def sty(j):
        return rdma(stat_y.at[me], stat_y.at[me], sty_ss.at[j - 1], sty_rs.at[me],
                    {"hid": lax.rem(me + j, nh)})

    def stx(j):
        return rdma(stat_x.at[vi], stat_x.at[vi], stx_ss.at[j - 1], stx_rs.at[vi],
                    {"vocab": lax.rem(vi + j, nv)})

    for j in range(1, nh):
        sty(j).start()
    for j in range(1, nh):
        s = lax.rem(me + j, nh)
        rdma(stat_y.at[s], stat_y.at[s], sty_ss.at[j - 1], sty_rs.at[s], to_up).wait_recv()
    m_me = stat_y[me, 0]
    m_g = stat_y[0, 0]
    for j in range(1, nh):
        m_g = jnp.maximum(m_g, stat_y[j, 0])
    zero = jnp.zeros_like(m_g)
    s_g, t_g, pre = zero, zero, zero
    for j in range(nh):
        f = jnp.exp(stat_y[j, 0] - m_g)
        s_j = stat_y[j, 1] * f
        pre = pre + jnp.where(j < me, s_j, 0.0)
        s_g = s_g + s_j
        t_g = t_g + stat_y[j, 2] * f
    stat_x[vi, 0] = m_g
    stat_x[vi, 1] = s_g
    stat_x[vi, 2] = t_g
    for j in range(1, nv):
        stx(j).start()
    for j in range(1, nv):
        s = lax.rem(vi + j, nv)
        rdma(stat_x.at[s], stat_x.at[s], stx_ss.at[j - 1], stx_rs.at[s], to_nxt).wait_recv()
    big = stat_x[0, 0]
    for j in range(1, nv):
        big = jnp.maximum(big, stat_x[j, 0])
    tot, low, hit = zero, zero, zero
    for j in range(nv):
        f = jnp.exp(stat_x[j, 0] - big)
        s_j = stat_x[j, 1] * f
        low = low + jnp.where(j < vi, s_j, 0.0)
        tot = tot + s_j
        hit = hit + stat_x[j, 2] * f
    scale_ref[...] = jnp.exp(m_me - big) / tot
    off_ref[...] = (low + pre * jnp.exp(m_g - big)) / tot
    ctgt_ref[...] = hit / tot

    for c in hy + leaf + direct + started:
        c.wait_send()

    def drain(i, _):
        for p in range(2):
            sum_copy(p, i).wait_send()
        out_copy(i).wait()
        return 0

    lax.fori_loop(0, nr, drain, 0)
    for j in range(1, nh):
        sty(j).wait_send()
    for j in range(1, nv):
        stx(j).wait_send()


def solution(mesh):
    nh = mesh.shape["hid"]
    nv = mesh.shape["vocab"]

    def local_step(h, w, temp, tgt):
        rows, depth = h.shape
        cols = w.shape[1]
        cb = cols // nh
        hc = cb // 2
        nr = rows // R
        f32, bf16 = jnp.float32, jnp.bfloat16
        dma = pltpu.SemaphoreType.DMA
        vm = pl.BlockSpec(memory_space=pltpu.VMEM)
        hbm = pl.BlockSpec(memory_space=pl.ANY)
        row_stat = jax.ShapeDtypeStruct((nr, R), f32)
        c, scale, off, ctgt = pl.pallas_call(
            functools.partial(head_kernel, nh, nv),
            name="head",
            out_shape=(jax.ShapeDtypeStruct((rows, cb), f32), row_stat, row_stat, row_stat),
            in_specs=[hbm, hbm, vm, vm],
            out_specs=(hbm, vm, vm, vm),
            scratch_shapes=[
                pltpu.VMEM((rows, depth), bf16),
                pltpu.VMEM((2, rows, depth), bf16),
                pltpu.VMEM((2, depth, hc), bf16),
                pltpu.VMEM((depth, cb), bf16),
                pltpu.VMEM((2, depth, hc), bf16),
                pltpu.VMEM((2, depth, hc), bf16),
                pltpu.VMEM((2, rows, hc), f32),
                pltpu.VMEM((2, rows, hc), f32),
                pltpu.VMEM((rows, cb), f32),
                pltpu.VMEM((nh, 3, nr, R), f32),
                pltpu.VMEM((nv, 3, nr, R), f32),
                dma((4,)), dma((2,)), dma((2,)), dma((2, 8)), dma((2, 8)),
                dma((2,)), dma((2,)), dma((2,)), dma((2,)),
                dma((2, nr)), dma((2, nr)),
                dma((nh - 1,)), dma((nh,)), dma((nv - 1,)), dma((nv,)),
                dma((nr,)),
            ],
            cost_estimate=pl.CostEstimate(
                flops=2 * rows * depth * cols, bytes_accessed=2 * depth * (rows + cols) + 4 * rows * cb,
                transcendentals=rows * cb),
            compiler_params=pltpu.CompilerParams(
                collective_id=0, has_side_effects=True, vmem_limit_bytes=60 * 1024 * 1024),
        )(h, w, temp.reshape(nr, R), tgt.reshape(nr, R))
        cdf = c * scale.reshape(rows)[:, None] + off.reshape(rows)[:, None]
        return cdf, ctgt.reshape(rows)

    return jax.shard_map(
        local_step, mesh=mesh,
        in_specs=(P("data", "hid"), P("hid", "vocab"), P("data"), P("data")),
        out_specs=(P("data", ("vocab", "hid")), P("data")), check_vma=False)
```

time: 409 us -> 146 us (0.36)
  blocking collectives: 167 us -> 0 us
  waiting for transfers between devices: 149 us -> 0 us
  Pallas kernels: 0 us -> 140 us
  local copies, waits for them, and re-layouts: 40.1 us -> 0.6 us
  matrix products: 19.3 us -> 0 us
  other arithmetic: 19.3 us -> 4.63 us
  between operations: 14.2 us -> 0.65 us
    reduce_scatter x1 -> x0, waiting for transfers between devices: 149 us -> none  [local_step(): lax.psum_scatter(part_logits, 'hid', scatter_dimension=1, tiled=True)]
    pallas_call x0 -> x1, Pallas kernels: none -> 140 us  [local_step(): pl.pallas_call(functools.partial(head_kernel, nh, nv), name='head', out_s...]
    psum x2 -> x0, blocking collectives: 92.7 us -> none  [the longest x1 48.3 us: local_step(): cdf_tgt = lax.psum(jnp.where(in_range, picked, 0.0), ('vocab', 'hid'))]
    pmax x1 -> x0, blocking collectives: 45.2 us -> none  [local_step(): glob_max = lax.pmax(jnp.max(logits, axis=1), ('vocab', 'hid'))]
    all_gather x2 -> x0, blocking collectives: 28.8 us -> none  [the longest x1 19.8 us: local_step(): vocab_tots = lax.all_gather(jnp.sum(hid_tots, axis=0), 'vocab')]
    dot_general x1 -> x0, matrix products: 19.3 us -> none  [local_step(): part_logits = jnp.dot(h_blk, w_blk, preferred_element_type=jnp.float32)]
    gather x1 -> x0, local copies, waits for them, and re-layouts: 16.8 us -> none  [local_step(): jnp.take_along_axis(cdf_blk, jnp.clip(local_pos, 0, local_cols - 1)[:, No...]
    another operation x5 -> x0, local copies, waits for them, and re-layouts: 13.2 us -> none
  transfers between devices with their start and end apart: 1 -> 0, of which waited for: 1 -> 0; matrix products, arithmetic and copies ran while one was open for 0% -> 0% of each run, Pallas kernels for 0% -> 0%
where the time goes in v1:
time: 146 us
  Pallas kernels  140 us (96%)
  other arithmetic  4.63 us (3%)
    pallas_call x1, Pallas kernels, local_step(): pl.pallas_call(functools.partial(head_kernel, nh, nv), name='head', out_s...  140 us
    add x1, other arithmetic, local_step(): cdf = c * scale.reshape(rows)[:, None] + off.reshape(rows)[:, None]  4.63 us

profile of v1, /device:TPU:97, one launch (start us, length us, event | category | flops | bytes accessed | tf_op | source)
XLA Modules:
  0.0 146.3 jit_solution(9668469588063937038)
XLA Ops:
  0.6 140.5 %head.1 = (f32[1024,1024]{1,0:T(8,128)}, f32[8,128]{1,0:T(8,128)}, f32[8,128]{1,0:T(8,128)}, f32[8,128]{1,0:T(8,128)}) custom-call(bf16[1024,1536]{1,0:T(8,128)(2,1)} %h_hbm.1, bf16[1536,4096]{1,0:T(8,128)(2,1)} %w_hbm.1, f32[8,128]{1,0:T(8,128)} %bitcast.8, s32[8,128]{1,0:T(8,128)} %bitcast.9), custom_call_target="tpu_custom_call" | custom-call | flops 12884901888 | bytes 19922944 | tf_op jit(solution)/shard_map/head/pallas_call | solution.py:289
  141.1 0.0 copy-start
  141.1 4.6 %multiply_add_fusion = f32[1024,1024]{1,0:T(8,128)} fusion(f32[1024,1024]{1,0:T(8,128)} %get-tuple-element.6, f32[1024]{0:T(1024)} %bitcast.6, f32[1024]{0:T(1024)} %bitcast.5), kind=kLoop, calls=%fused_computation | loop fusion | flops 2097152 | bytes 8396800 | tf_op jit(solution)/shard_map/add | solution.py:319
  145.7 0.0 copy-done
  145.7 0.6 copy.7
Async XLA Ops:
  141.1 4.6 %copy-start = (f32[8,128]{1,0:T(8,128)S(1)}, f32[8,128]{1,0:T(8,128)}, u32[]{:S(2)}) copy-start(f32[8,128]{1,0:T(8,128)} %get-tuple-element.9) | copy-start | bytes 12292

commit v2 on v1

--- a/solution.py
+++ b/solution.py
@@ -13,12 +13,12 @@
 TRI = 256
 
 
-def head_kernel(nh, nv, h_hbm, w_hbm, temp_ref, tgt_ref,
-                c_hbm, scale_ref, off_ref, ctgt_ref,
-                h_own, h_nb, w_sum, w_own, w_leaf, w_dir, s_send, s_recv, z_buf,
-                stat_y, stat_x,
+def head_kernel(nh, nv, h_hbm, w_hbm, temp_hbm, tgt_hbm,
+                z_buf, scale_ref, off_ref, hit_ref,
+                h_own, h_nb, w_sum, w_own, w_leaf, w_dir, s_send, s_recv, temp_ref, tgt_ref,
+                sy_a, sx_a, sy_b, sx_b,
                 ld_sem, hy_ss, hy_rs, hx_ss, hx_rs, leaf_ss, leaf_rs, dir_ss, dir_rs,
-                sum_ss, sum_rs, sty_ss, sty_rs, stx_ss, stx_rs, out_sem):
+                sum_ss, sum_rs, sty_ss, sty_rs, stx_ss, stx_rs):
     rows, depth = h_hbm.shape
     cb = w_hbm.shape[1] // nh
     hc = cb // 2
@@ -53,6 +53,8 @@
         pltpu.make_async_copy(w_hbm.at[:, tok(up, 1)], w_sum.at[1], ld_sem.at[2]),
         pltpu.make_async_copy(
             w_hbm.at[:, pl.ds(pl.multiple_of(me * cb, LANES), cb)], w_own, ld_sem.at[3]),
+        pltpu.make_async_copy(temp_hbm, temp_ref, ld_sem.at[4]),
+        pltpu.make_async_copy(tgt_hbm, tgt_ref, ld_sem.at[5]),
     ]
     for c in loads:
         c.start()
@@ -68,12 +70,13 @@
 
     to_dn, to_up = {"hid": dn}, {"hid": up}
     mine = rws(vi * piece, piece)
-    hy = [rdma(h_hbm.at[mine], h_nb.at[0, mine], hy_ss.at[0], hy_rs.at[0], to_dn),
-          rdma(h_hbm.at[mine], h_nb.at[1, mine], hy_ss.at[1], hy_rs.at[1], to_up)]
+    hy = [rdma(h_own.at[mine], h_nb.at[0, mine], hy_ss.at[0], hy_rs.at[0], to_dn),
+          rdma(h_own.at[mine], h_nb.at[1, mine], hy_ss.at[1], hy_rs.at[1], to_up)]
     leaf = [rdma(w_hbm.at[:, tok(far, 0)], w_leaf.at[0], leaf_ss.at[0], leaf_rs.at[0], to_dn),
             rdma(w_hbm.at[:, tok(far, 1)], w_leaf.at[1], leaf_ss.at[1], leaf_rs.at[1], to_up)]
     direct = [rdma(w_hbm.at[:, tok(up, 0)], w_dir.at[0], dir_ss.at[0], dir_rs.at[0], to_up),
               rdma(w_hbm.at[:, tok(dn, 1)], w_dir.at[1], dir_ss.at[1], dir_rs.at[1], to_dn)]
+    loads[0].wait()
     for c in hy + leaf:
         c.start()
 
@@ -99,7 +102,7 @@
     for c in direct:
         c.start()
 
-    for c in loads:
+    for c in loads[1:]:
         c.wait()
 
     def own(i, _):
@@ -159,14 +162,10 @@
     lane = lax.broadcasted_iota(jnp.int32, (R, LANES), 1)
     first_tok = ((vi * nh + me) * cb).astype(jnp.float32)
 
-    def out_copy(i):
-        at = rws(i * R, R)
-        return pltpu.make_async_copy(z_buf.at[at], c_hbm.at[at], out_sem.at[i])
-
     def by_row(v):
         return jnp.broadcast_to(v, (LANES, R)).T
 
-    def softmax(i, _):
+    def softmax(i, sy, k):
         at = rws(i * R, R)
         for p in range(2):
             sl = slice(p * hc, (p + 1) * hc)
@@ -199,61 +198,81 @@
                  + jnp.dot(e1, tri, preferred_element_type=jnp.float32)) + carry
             z_buf[at, b * TRI:(b + 1) * TRI] = c
             carry = c[:, TRI - 1:TRI]
-        out_copy(i).start()
         t = jnp.sum(picked, axis=1, keepdims=True)
         st = jnp.where(lane == 0, m, jnp.where(lane == 1, carry, jnp.where(lane == 2, t, 0.0))).T
-        for k in range(3):
-            stat_y[me, k, pl.ds(i, 1)] = st[k:k + 1]
-        return 0
-
-    lax.fori_loop(0, nr, softmax, 0)
-
-    def sty(j):
-        return rdma(stat_y.at[me], stat_y.at[me], sty_ss.at[j - 1], sty_rs.at[me],
+        for q in range(3):
+            sy[me, q, pl.ds(k, 1)] = st[q:q + 1]
+
+    def sty(g, j):
+        sy = (sy_a, sy_b)[g]
+        return rdma(sy.at[me], sy.at[me], sty_ss.at[g, j - 1], sty_rs.at[g, me],
                     {"hid": lax.rem(me + j, nh)})
 
-    def stx(j):
-        return rdma(stat_x.at[vi], stat_x.at[vi], stx_ss.at[j - 1], stx_rs.at[vi],
+    def stx(g, j):
+        sx = (sx_a, sx_b)[g]
+        return rdma(sx.at[vi], sx.at[vi], stx_ss.at[g, j - 1], stx_rs.at[g, vi],
                     {"vocab": lax.rem(vi + j, nv)})
 
-    for j in range(1, nh):
-        sty(j).start()
-    for j in range(1, nh):
-        s = lax.rem(me + j, nh)
-        rdma(stat_y.at[s], stat_y.at[s], sty_ss.at[j - 1], sty_rs.at[s], to_up).wait_recv()
-    m_me = stat_y[me, 0]
-    m_g = stat_y[0, 0]
-    for j in range(1, nh):
-        m_g = jnp.maximum(m_g, stat_y[j, 0])
-    zero = jnp.zeros_like(m_g)
-    s_g, t_g, pre = zero, zero, zero
-    for j in range(nh):
-        f = jnp.exp(stat_y[j, 0] - m_g)
-        s_j = stat_y[j, 1] * f
-        pre = pre + jnp.where(j < me, s_j, 0.0)
-        s_g = s_g + s_j
-        t_g = t_g + stat_y[j, 2] * f
-    stat_x[vi, 0] = m_g
-    stat_x[vi, 1] = s_g
-    stat_x[vi, 2] = t_g
-    for j in range(1, nv):
-        stx(j).start()
-    for j in range(1, nv):
-        s = lax.rem(vi + j, nv)
-        rdma(stat_x.at[s], stat_x.at[s], stx_ss.at[j - 1], stx_rs.at[s], to_nxt).wait_recv()
-    big = stat_x[0, 0]
-    for j in range(1, nv):
-        big = jnp.maximum(big, stat_x[j, 0])
-    tot, low, hit = zero, zero, zero
-    for j in range(nv):
-        f = jnp.exp(stat_x[j, 0] - big)
-        s_j = stat_x[j, 1] * f
-        low = low + jnp.where(j < vi, s_j, 0.0)
-        tot = tot + s_j
-        hit = hit + stat_x[j, 2] * f
-    scale_ref[...] = jnp.exp(m_me - big) / tot
-    off_ref[...] = (low + pre * jnp.exp(m_g - big)) / tot
-    ctgt_ref[...] = hit / tot
+    def send_y(g):
+        for j in range(1, nh):
+            sty(g, j).start()
+
+    def merge_y(g):
+        sy, sx = (sy_a, sy_b)[g], (sx_a, sx_b)[g]
+        for j in range(1, nh):
+            s = lax.rem(me + j, nh)
+            rdma(sy.at[s], sy.at[s], sty_ss.at[g, j - 1], sty_rs.at[g, s], to_up).wait_recv()
+        m_g = sy[0, 0]
+        for j in range(1, nh):
+            m_g = jnp.maximum(m_g, sy[j, 0])
+        zero = jnp.zeros_like(m_g)
+        s_g, t_g, pre = zero, zero, zero
+        for j in range(nh):
+            f = jnp.exp(sy[j, 0] - m_g)
+            s_j = sy[j, 1] * f
+            pre = pre + jnp.where(j < me, s_j, 0.0)
+            s_g = s_g + s_j
+            t_g = t_g + sy[j, 2] * f
+        sx[vi, 0] = m_g
+        sx[vi, 1] = s_g
+        sx[vi, 2] = t_g
+        for j in range(1, nv):
+            stx(g, j).start()
+        return m_g, pre
+
+    def merge_x(g, m_g, pre, out):
+        sy, sx = (sy_a, sy_b)[g], (sx_a, sx_b)[g]
+        for j in range(1, nv):
+            s = lax.rem(vi + j, nv)
+            rdma(sx.at[s], sx.at[s], stx_ss.at[g, j - 1], stx_rs.at[g, s], to_nxt).wait_recv()
+        big = sx[0, 0]
+        for j in range(1, nv):
+            big = jnp.maximum(big, sx[j, 0])
+        zero = jnp.zeros_like(big)
+        tot, low, hit = zero, zero, zero
+        for j in range(nv):
+            f = jnp.exp(sx[j, 0] - big)
+            s_j = sx[j, 1] * f
+            low = low + jnp.where(j < vi, s_j, 0.0)
+            tot = tot + s_j
+            hit = hit + sx[j, 2] * f
+        scale_ref[out] = jnp.exp(sy[me, 0] - big) / tot
+        off_ref[out] = (low + pre * jnp.exp(m_g - big)) / tot
+        hit_ref[out] = hit / tot
+
+    last = nr - 1
+    for q in range(3):
+        sy_a[me, q, last:nr] = jnp.zeros((1, R), jnp.float32)
+
+    def block(i, _):
+        softmax(i, sy_a, i)
+        return 0
+
+    lax.fori_loop(0, last, block, 0)
+    send_y(0)
+    softmax(last, sy_b, 0)
+    send_y(1)
+    got_a = merge_y(0)
 
     for c in hy + leaf + direct + started:
         c.wait_send()
@@ -261,14 +280,47 @@
     def drain(i, _):
         for p in range(2):
             sum_copy(p, i).wait_send()
+        return 0
+
+    lax.fori_loop(0, nr, drain, 0)
+    got_b = merge_y(1)
+    merge_x(0, *got_a, slice(None))
+    merge_x(1, *got_b, slice(last, nr))
+    for g in range(2):
+        for j in range(1, nh):
+            sty(g, j).wait_send()
+        for j in range(1, nv):
+            stx(g, j).wait_send()
+
+
+def final_kernel(c_ref, scale_ref, off_ref, hit_ref, out_hbm, hit_out, buf, sem):
+    nr = scale_ref.shape[0]
+
+    def by_row(v):
+        return jnp.broadcast_to(v, (LANES, R)).T
+
+    def out_copy(i):
+        at = pl.ds(pl.multiple_of(i * R, R), R)
+        return pltpu.make_async_copy(buf.at[at], out_hbm.at[at], sem.at[i])
+
+    def block(i, _):
+        a = by_row(scale_ref[pl.ds(i, 1)])
+        b = by_row(off_ref[pl.ds(i, 1)])
+        at = pl.ds(pl.multiple_of(i * R, R), R)
+        for j in range(c_ref.shape[1] // LANES):
+            sl = slice(j * LANES, (j + 1) * LANES)
+            buf[at, sl] = c_ref[at, sl] * a + b
+        out_copy(i).start()
+        return 0
+
+    lax.fori_loop(0, nr, block, 0)
+    hit_out[...] = hit_ref[...]
+
+    def drain(i, _):
         out_copy(i).wait()
         return 0
 
     lax.fori_loop(0, nr, drain, 0)
-    for j in range(1, nh):
-        sty(j).wait_send()
-    for j in range(1, nv):
-        stx(j).wait_send()
 
 
 def solution(mesh):
@@ -284,14 +336,15 @@
         f32, bf16 = jnp.float32, jnp.bfloat16
         dma = pltpu.SemaphoreType.DMA
         vm = pl.BlockSpec(memory_space=pltpu.VMEM)
-        hbm = pl.BlockSpec(memory_space=pl.ANY)
+        hbm = pl.BlockSpec(memory_space=pltpu.HBM)
         row_stat = jax.ShapeDtypeStruct((nr, R), f32)
-        c, scale, off, ctgt = pl.pallas_call(
+        table = jax.ShapeDtypeStruct((rows, cb), f32)
+        c, scale, off, hit = pl.pallas_call(
             functools.partial(head_kernel, nh, nv),
             name="head",
-            out_shape=(jax.ShapeDtypeStruct((rows, cb), f32), row_stat, row_stat, row_stat),
-            in_specs=[hbm, hbm, vm, vm],
-            out_specs=(hbm, vm, vm, vm),
+            out_shape=(table, row_stat, row_stat, row_stat),
+            in_specs=[hbm, hbm, hbm, hbm],
+            out_specs=(vm, vm, vm, vm),
             scratch_shapes=[
                 pltpu.VMEM((rows, depth), bf16),
                 pltpu.VMEM((2, rows, depth), bf16),
@@ -301,22 +354,33 @@
                 pltpu.VMEM((2, depth, hc), bf16),
                 pltpu.VMEM((2, rows, hc), f32),
                 pltpu.VMEM((2, rows, hc), f32),
-                pltpu.VMEM((rows, cb), f32),
+                pltpu.VMEM((nr, R), f32),
+                pltpu.VMEM((nr, R), jnp.int32),
                 pltpu.VMEM((nh, 3, nr, R), f32),
                 pltpu.VMEM((nv, 3, nr, R), f32),
-                dma((4,)), dma((2,)), dma((2,)), dma((2, 8)), dma((2, 8)),
+                pltpu.VMEM((nh, 3, 1, R), f32),
+                pltpu.VMEM((nv, 3, 1, R), f32),
+                dma((6,)), dma((2,)), dma((2,)), dma((2, 8)), dma((2, 8)),
                 dma((2,)), dma((2,)), dma((2,)), dma((2,)),
                 dma((2, nr)), dma((2, nr)),
-                dma((nh - 1,)), dma((nh,)), dma((nv - 1,)), dma((nv,)),
-                dma((nr,)),
+                dma((2, nh - 1)), dma((2, nh)), dma((2, nv - 1)), dma((2, nv)),
             ],
             cost_estimate=pl.CostEstimate(
                 flops=2 * rows * depth * cols, bytes_accessed=2 * depth * (rows + cols) + 4 * rows * cb,
                 transcendentals=rows * cb),
             compiler_params=pltpu.CompilerParams(
-                collective_id=0, has_side_effects=True, vmem_limit_bytes=60 * 1024 * 1024),
-        )(h, w, temp.reshape(nr, R), tgt.reshape(nr, R))
-        cdf = c * scale.reshape(rows)[:, None] + off.reshape(rows)[:, None]
+                collective_id=0, has_side_effects=True, vmem_limit_bytes=44 * 1024 * 1024),
+        )(*[pltpu.with_memory_space_constraint(x, pltpu.HBM)
+            for x in (h, w, temp.reshape(nr, R), tgt.reshape(nr, R))])
+        cdf, ctgt = pl.pallas_call(
+            final_kernel,
+            name="final",
+            out_shape=(table, row_stat),
+            in_specs=[vm, vm, vm, vm],
+            out_specs=(hbm, vm),
+            scratch_shapes=[pltpu.VMEM((rows, cb), f32), dma((nr,))],
+            compiler_params=pltpu.CompilerParams(vmem_limit_bytes=16 * 1024 * 1024),
+        )(c, scale, off, hit)
         return cdf, ctgt.reshape(rows)
 
     return jax.shard_map(

time: 146 us -> 143 us (0.979)
  other arithmetic: 4.63 us -> 0 us
  Pallas kernels: 140 us -> 142 us
    add x1 -> x0, other arithmetic: 4.63 us -> none  [local_step(): cdf = c * scale.reshape(rows)[:, None] + off.reshape(rows)[:, None]]
    pallas_call x0 -> x1, Pallas kernels: none -> 2.77 us  [local_step(): pl.pallas_call(final_kernel, name='final', out_shape=(table, row_stat), i...]
where the time goes in v2:
time: 143 us
  Pallas kernels  142 us (99%)
    pallas_call x1, Pallas kernels, local_step(): pl.pallas_call(functools.partial(head_kernel, nh, nv), name='head', out_s...  139 us

profile of v2, /device:TPU:97, one launch (start us, length us, event | category | flops | bytes accessed | tf_op | source)
XLA Modules:
  0.0 142.7 jit_solution(10775815228757260888)
XLA Ops:
  0.6 139.3 %head.1 = (f32[1024,1024]{1,0:T(8,128)S(1)}, f32[8,128]{1,0:T(8,128)S(1)}, f32[8,128]{1,0:T(8,128)S(1)}, f32[8,128]{1,0:T(8,128)S(1)}) custom-call(bf16[1024,1536]{1,0:T(8,128)(2,1)} %h_hbm.1, bf16[1536,4096]{1,0:T(8,128)(2,1)} %w_hbm.1, f32[8,128]{1,0:T(8,128)} %bitcast.3, s32[8,128]{1,0:T(8,128)} %bitcast.4), custom_call_target="tpu_custom_call" | custom-call | flops 12884901888 | bytes 19922944 | tf_op jit(solution)/shard_map/head/pallas_call | solution.py:342
  139.9 2.8 %final.1 = (f32[1024,1024]{1,0:T(8,128)}, f32[8,128]{1,0:T(8,128)}) custom-call(f32[1024,1024]{1,0:T(8,128)S(1)} %get-tuple-element.8.c_ref, f32[8,128]{1,0:T(8,128)S(1)} %get-tuple-element.9.scale_ref, f32[8,128]{1,0:T(8,128)S(1)} %get-tuple-element.10.off_ref, f32[8,128]{1,0:T(8,128)S(1)} %get-tuple-element.11.hit_ref), custom_call_target="tpu_custom_call" | custom-call | tf_op jit(solution)/shard_map/final/pallas_call | solution.py:375

commit v3 on v2

--- a/solution.py
+++ b/solution.py
@@ -10,15 +10,16 @@
 MESH = pl.DeviceIdType.MESH
 R = 128
 LANES = 128
+NC = 1
 TRI = 256
 
 
 def head_kernel(nh, nv, h_hbm, w_hbm, temp_hbm, tgt_hbm,
-                z_buf, scale_ref, off_ref, hit_ref,
+                z_buf, hit_ref,
                 h_own, h_nb, w_sum, w_own, w_leaf, w_dir, s_send, s_recv, temp_ref, tgt_ref,
-                sy_a, sx_a, sy_b, sx_b,
+                sy_a, sx_a, s_all,
                 ld_sem, hy_ss, hy_rs, hx_ss, hx_rs, leaf_ss, leaf_rs, dir_ss, dir_rs,
-                sum_ss, sum_rs, sty_ss, sty_rs, stx_ss, stx_rs):
+                sum_ss, sum_rs, sty_ss, sty_rs, stx_ss, stx_rs, all_ss, all_rs):
     rows, depth = h_hbm.shape
     cb = w_hbm.shape[1] // nh
     hc = cb // 2
@@ -165,7 +166,13 @@
     def by_row(v):
         return jnp.broadcast_to(v, (LANES, R)).T
 
-    def softmax(i, sy, k):
+    def finish(start, scale, off):
+        a, b = by_row(scale), by_row(off)
+        for j in range(cb // LANES):
+            sl = slice(j * LANES, (j + 1) * LANES)
+            z_buf[start:start + R, sl] = z_buf[start:start + R, sl] * a + b
+
+    def softmax(i, sy, slot, k):
         at = rws(i * R, R)
         for p in range(2):
             sl = slice(p * hc, (p + 1) * hc)
@@ -201,78 +208,113 @@
         t = jnp.sum(picked, axis=1, keepdims=True)
         st = jnp.where(lane == 0, m, jnp.where(lane == 1, carry, jnp.where(lane == 2, t, 0.0))).T
         for q in range(3):
-            sy[me, q, pl.ds(k, 1)] = st[q:q + 1]
-
-    def sty(g, j):
-        sy = (sy_a, sy_b)[g]
-        return rdma(sy.at[me], sy.at[me], sty_ss.at[g, j - 1], sty_rs.at[g, me],
+            sy[slot, q, pl.ds(k, 1)] = st[q:q + 1]
+
+    def sty(j):
+        return rdma(sy_a.at[me], sy_a.at[me], sty_ss.at[j - 1], sty_rs.at[me],
                     {"hid": lax.rem(me + j, nh)})
 
-    def stx(g, j):
-        sx = (sx_a, sx_b)[g]
-        return rdma(sx.at[vi], sx.at[vi], stx_ss.at[g, j - 1], stx_rs.at[g, vi],
+    def stx(j):
+        return rdma(sx_a.at[vi], sx_a.at[vi], stx_ss.at[j - 1], stx_rs.at[vi],
                     {"vocab": lax.rem(vi + j, nv)})
 
-    def send_y(g):
-        for j in range(1, nh):
-            sty(g, j).start()
-
-    def merge_y(g):
-        sy, sx = (sy_a, sy_b)[g], (sx_a, sx_b)[g]
+    def merge_y():
         for j in range(1, nh):
             s = lax.rem(me + j, nh)
-            rdma(sy.at[s], sy.at[s], sty_ss.at[g, j - 1], sty_rs.at[g, s], to_up).wait_recv()
-        m_g = sy[0, 0]
+            rdma(sy_a.at[s], sy_a.at[s], sty_ss.at[j - 1], sty_rs.at[s], to_up).wait_recv()
+        m_g = sy_a[0, 0]
         for j in range(1, nh):
-            m_g = jnp.maximum(m_g, sy[j, 0])
+            m_g = jnp.maximum(m_g, sy_a[j, 0])
         zero = jnp.zeros_like(m_g)
         s_g, t_g, pre = zero, zero, zero
         for j in range(nh):
-            f = jnp.exp(sy[j, 0] - m_g)
-            s_j = sy[j, 1] * f
+            f = jnp.exp(sy_a[j, 0] - m_g)
+            s_j = sy_a[j, 1] * f
             pre = pre + jnp.where(j < me, s_j, 0.0)
             s_g = s_g + s_j
-            t_g = t_g + sy[j, 2] * f
-        sx[vi, 0] = m_g
-        sx[vi, 1] = s_g
-        sx[vi, 2] = t_g
+            t_g = t_g + sy_a[j, 2] * f
+        sx_a[vi, 0] = m_g
+        sx_a[vi, 1] = s_g
+        sx_a[vi, 2] = t_g
         for j in range(1, nv):
-            stx(g, j).start()
+            stx(j).start()
         return m_g, pre
 
-    def merge_x(g, m_g, pre, out):
-        sy, sx = (sy_a, sy_b)[g], (sx_a, sx_b)[g]
+    def merge_x(m_g, pre):
         for j in range(1, nv):
             s = lax.rem(vi + j, nv)
-            rdma(sx.at[s], sx.at[s], stx_ss.at[g, j - 1], stx_rs.at[g, s], to_nxt).wait_recv()
-        big = sx[0, 0]
+            rdma(sx_a.at[s], sx_a.at[s], stx_ss.at[j - 1], stx_rs.at[s], to_nxt).wait_recv()
+        big = sx_a[0, 0]
         for j in range(1, nv):
-            big = jnp.maximum(big, sx[j, 0])
+            big = jnp.maximum(big, sx_a[j, 0])
         zero = jnp.zeros_like(big)
         tot, low, hit = zero, zero, zero
         for j in range(nv):
-            f = jnp.exp(sx[j, 0] - big)
-            s_j = sx[j, 1] * f
+            f = jnp.exp(sx_a[j, 0] - big)
+            s_j = sx_a[j, 1] * f
             low = low + jnp.where(j < vi, s_j, 0.0)
             tot = tot + s_j
-            hit = hit + sx[j, 2] * f
-        scale_ref[out] = jnp.exp(sy[me, 0] - big) / tot
-        off_ref[out] = (low + pre * jnp.exp(m_g - big)) / tot
-        hit_ref[out] = hit / tot
+            hit = hit + sx_a[j, 2] * f
+        scale = jnp.exp(sy_a[me, 0] - big) / tot
+        off = (low + pre * jnp.exp(m_g - big)) / tot
+        hit_ref[...] = hit / tot
+        for i in range(last):
+            finish(i * R, scale[i:i + 1], off[i:i + 1])
+
+    nd = nv * nh
+    own_slot = vi * nh + me
+
+    def peer(k):
+        return lax.rem(vi + k // nh, nv), lax.rem(me + lax.rem(k, nh), nh)
+
+    def sta(k):
+        v, h = peer(k)
+        return rdma(s_all.at[own_slot], s_all.at[own_slot], all_ss.at[k], all_rs.at[own_slot],
+                    {"hid": h, "vocab": v})
+
+    def send_all(k, _):
+        sta(k).start()
+        return 0
+
+    def hear_all(k, _):
+        v, h = peer(k)
+        s = v * nh + h
+        rdma(s_all.at[s], s_all.at[s], all_ss.at[k], all_rs.at[s], to_up).wait_recv()
+        return 0
+
+    def sent_all(k, _):
+        sta(k).wait_send()
+        return 0
+
+    def merge_all():
+        big = s_all[0, 0]
+        for j in range(1, nd):
+            big = jnp.maximum(big, s_all[j, 0])
+        zero = jnp.zeros_like(big)
+        tot, low, hit = zero, zero, zero
+        for j in range(nd):
+            f = jnp.exp(s_all[j, 0] - big)
+            s_j = s_all[j, 1] * f
+            low = low + jnp.where(j < own_slot, s_j, 0.0)
+            tot = tot + s_j
+            hit = hit + s_all[j, 2] * f
+        hit_ref[last:nr] = hit / tot
+        finish(last * R, jnp.exp(s_all[own_slot, 0] - big) / tot, low / tot)
 
     last = nr - 1
     for q in range(3):
         sy_a[me, q, last:nr] = jnp.zeros((1, R), jnp.float32)
 
     def block(i, _):
-        softmax(i, sy_a, i)
+        softmax(i, sy_a, me, i)
         return 0
 
     lax.fori_loop(0, last, block, 0)
-    send_y(0)
-    softmax(last, sy_b, 0)
-    send_y(1)
-    got_a = merge_y(0)
+    for j in range(1, nh):
+        sty(j).start()
+    softmax(last, s_all, own_slot, 0)
+    lax.fori_loop(1, nd, send_all, 0)
+    got = merge_y()
 
     for c in hy + leaf + direct + started:
         c.wait_send()
@@ -283,44 +325,26 @@
         return 0
 
     lax.fori_loop(0, nr, drain, 0)
-    got_b = merge_y(1)
-    merge_x(0, *got_a, slice(None))
-    merge_x(1, *got_b, slice(last, nr))
-    for g in range(2):
-        for j in range(1, nh):
-            sty(g, j).wait_send()
-        for j in range(1, nv):
-            stx(g, j).wait_send()
-
-
-def final_kernel(c_ref, scale_ref, off_ref, hit_ref, out_hbm, hit_out, buf, sem):
-    nr = scale_ref.shape[0]
-
-    def by_row(v):
-        return jnp.broadcast_to(v, (LANES, R)).T
-
-    def out_copy(i):
-        at = pl.ds(pl.multiple_of(i * R, R), R)
-        return pltpu.make_async_copy(buf.at[at], out_hbm.at[at], sem.at[i])
-
-    def block(i, _):
-        a = by_row(scale_ref[pl.ds(i, 1)])
-        b = by_row(off_ref[pl.ds(i, 1)])
-        at = pl.ds(pl.multiple_of(i * R, R), R)
-        for j in range(c_ref.shape[1] // LANES):
-            sl = slice(j * LANES, (j + 1) * LANES)
-            buf[at, sl] = c_ref[at, sl] * a + b
-        out_copy(i).start()
-        return 0
-
-    lax.fori_loop(0, nr, block, 0)
-    hit_out[...] = hit_ref[...]
-
-    def drain(i, _):
-        out_copy(i).wait()
-        return 0
-
-    lax.fori_loop(0, nr, drain, 0)
+    merge_x(*got)
+    lax.fori_loop(1, nd, hear_all, 0)
+    merge_all()
+    for j in range(1, nh):
+        sty(j).wait_send()
+    for j in range(1, nv):
+        stx(j).wait_send()
+    lax.fori_loop(1, nd, sent_all, 0)
+
+
+def store_kernel(nc, c_ref, hit_ref, out_hbm, hit_hbm, sem):
+    rows = c_ref.shape[0] // nc
+    copies = [pltpu.make_async_copy(c_ref.at[i * rows:(i + 1) * rows],
+                                    out_hbm.at[i * rows:(i + 1) * rows], sem.at[i])
+              for i in range(nc)]
+    copies.append(pltpu.make_async_copy(hit_ref, hit_hbm, sem.at[nc]))
+    for c in copies:
+        c.start()
+    for c in copies:
+        c.wait()
 
 
 def solution(mesh):
@@ -338,13 +362,13 @@
         vm = pl.BlockSpec(memory_space=pltpu.VMEM)
         hbm = pl.BlockSpec(memory_space=pltpu.HBM)
         row_stat = jax.ShapeDtypeStruct((nr, R), f32)
-        table = jax.ShapeDtypeStruct((rows, cb), f32)
-        c, scale, off, hit = pl.pallas_call(
+        cdf_out = jax.ShapeDtypeStruct((rows, cb), f32)
+        table, hit = pl.pallas_call(
             functools.partial(head_kernel, nh, nv),
             name="head",
-            out_shape=(table, row_stat, row_stat, row_stat),
+            out_shape=(cdf_out, row_stat),
             in_specs=[hbm, hbm, hbm, hbm],
-            out_specs=(vm, vm, vm, vm),
+            out_specs=(vm, vm),
             scratch_shapes=[
                 pltpu.VMEM((rows, depth), bf16),
                 pltpu.VMEM((2, rows, depth), bf16),
@@ -358,12 +382,11 @@
                 pltpu.VMEM((nr, R), jnp.int32),
                 pltpu.VMEM((nh, 3, nr, R), f32),
                 pltpu.VMEM((nv, 3, nr, R), f32),
-                pltpu.VMEM((nh, 3, 1, R), f32),
-                pltpu.VMEM((nv, 3, 1, R), f32),
+                pltpu.VMEM((nh * nv, 3, 1, R), f32),
                 dma((6,)), dma((2,)), dma((2,)), dma((2, 8)), dma((2, 8)),
                 dma((2,)), dma((2,)), dma((2,)), dma((2,)),
                 dma((2, nr)), dma((2, nr)),
-                dma((2, nh - 1)), dma((2, nh)), dma((2, nv - 1)), dma((2, nv)),
+                dma((nh - 1,)), dma((nh,)), dma((nv - 1,)), dma((nv,)), dma((nh * nv,)), dma((nh * nv,)),
             ],
             cost_estimate=pl.CostEstimate(
                 flops=2 * rows * depth * cols, bytes_accessed=2 * depth * (rows + cols) + 4 * rows * cb,
@@ -373,14 +396,14 @@
         )(*[pltpu.with_memory_space_constraint(x, pltpu.HBM)
             for x in (h, w, temp.reshape(nr, R), tgt.reshape(nr, R))])
         cdf, ctgt = pl.pallas_call(
-            final_kernel,
-            name="final",
-            out_shape=(table, row_stat),
-            in_specs=[vm, vm, vm, vm],
-            out_specs=(hbm, vm),
-            scratch_shapes=[pltpu.VMEM((rows, cb), f32), dma((nr,))],
-            compiler_params=pltpu.CompilerParams(vmem_limit_bytes=16 * 1024 * 1024),
-        )(c, scale, off, hit)
+            functools.partial(store_kernel, NC),
+            name="store",
+            out_shape=(cdf_out, row_stat),
+            in_specs=[vm, vm],
+            out_specs=(hbm, hbm),
+            scratch_shapes=[dma((NC + 1,))],
+            compiler_params=pltpu.CompilerParams(vmem_limit_bytes=4 * 1024 * 1024),
+        )(table, hit)
         return cdf, ctgt.reshape(rows)
 
     return jax.shard_map(

time: 143 us -> 142 us (level)
  no operation moved by 1% of the time
where the time goes in v3:
time: 142 us
  Pallas kernels  141 us (99%)
    pallas_call x1, Pallas kernels, local_step(): pl.pallas_call(functools.partial(head_kernel, nh, nv), name='head', out_s...  139 us

profile of v3, /device:TPU:97, one launch (start us, length us, event | category | flops | bytes accessed | tf_op | source)
XLA Modules:
  0.0 141.9 jit_solution(5328163458213226360)
XLA Ops:
  0.6 139.3 %head.1 = (f32[1024,1024]{1,0:T(8,128)S(1)}, f32[8,128]{1,0:T(8,128)S(1)}) custom-call(bf16[1024,1536]{1,0:T(8,128)(2,1)} %h_hbm.1, bf16[1536,4096]{1,0:T(8,128)(2,1)} %w_hbm.1, f32[8,128]{1,0:T(8,128)} %bitcast.3, s32[8,128]{1,0:T(8,128)} %bitcast.4), custom_call_target="tpu_custom_call" | custom-call | flops 12884901888 | bytes 19922944 | tf_op jit(solution)/shard_map/head/pallas_call | solution.py:366
  139.9 2.0 %store.1 = (f32[1024,1024]{1,0:T(8,128)}, f32[8,128]{1,0:T(8,128)}) custom-call(f32[1024,1024]{1,0:T(8,128)S(1)} %get-tuple-element.6.c_ref, f32[8,128]{1,0:T(8,128)S(1)} %get-tuple-element.7.hit_ref), custom_call_target="tpu_custom_call" | custom-call | tf_op jit(solution)/shard_map/store/pallas_call | solution.py:398

commit v4 on v3

--- a/solution.py
+++ b/solution.py
@@ -11,13 +11,14 @@
 R = 128
 LANES = 128
 NC = 1
+NB = 2
 TRI = 256
 
 
 def head_kernel(nh, nv, h_hbm, w_hbm, temp_hbm, tgt_hbm,
                 z_buf, hit_ref,
                 h_own, h_nb, w_sum, w_own, w_leaf, w_dir, s_send, s_recv, temp_ref, tgt_ref,
-                sy_a, sx_a, s_all,
+                sx_a, sy_out, sy_a, s_all,
                 ld_sem, hy_ss, hy_rs, hx_ss, hx_rs, leaf_ss, leaf_rs, dir_ss, dir_rs,
                 sum_ss, sum_rs, sty_ss, sty_rs, stx_ss, stx_rs, all_ss, all_rs):
     rows, depth = h_hbm.shape
@@ -71,13 +72,12 @@
 
     to_dn, to_up = {"hid": dn}, {"hid": up}
     mine = rws(vi * piece, piece)
-    hy = [rdma(h_own.at[mine], h_nb.at[0, mine], hy_ss.at[0], hy_rs.at[0], to_dn),
-          rdma(h_own.at[mine], h_nb.at[1, mine], hy_ss.at[1], hy_rs.at[1], to_up)]
+    hy = [rdma(h_hbm.at[mine], h_nb.at[0, mine], hy_ss.at[0], hy_rs.at[0], to_dn),
+          rdma(h_hbm.at[mine], h_nb.at[1, mine], hy_ss.at[1], hy_rs.at[1], to_up)]
     leaf = [rdma(w_hbm.at[:, tok(far, 0)], w_leaf.at[0], leaf_ss.at[0], leaf_rs.at[0], to_dn),
             rdma(w_hbm.at[:, tok(far, 1)], w_leaf.at[1], leaf_ss.at[1], leaf_rs.at[1], to_up)]
     direct = [rdma(w_hbm.at[:, tok(up, 0)], w_dir.at[0], dir_ss.at[0], dir_rs.at[0], to_up),
               rdma(w_hbm.at[:, tok(dn, 1)], w_dir.at[1], dir_ss.at[1], dir_rs.at[1], to_dn)]
-    loads[0].wait()
     for c in hy + leaf:
         c.start()
 
@@ -103,7 +103,7 @@
     for c in direct:
         c.start()
 
-    for c in loads[1:]:
+    for c in loads:
         c.wait()
 
     def own(i, _):
@@ -191,11 +191,24 @@
             zs.append(z)
             m = z if m is None else jnp.maximum(m, z)
         m = jnp.max(m, axis=1, keepdims=True)
-        carry = jnp.zeros((R, 1), jnp.float32)
+        total = jnp.zeros((R, TRI), jnp.float32)
         picked = jnp.zeros((R, TRI), jnp.float32)
         for b in range(cb // TRI):
             e = jnp.exp(zs[b] - m)
+            z_buf[at, b * TRI:(b + 1) * TRI] = e
+            total = total + e
             picked = picked + jnp.where(col + float(b * TRI) <= tgt, e, 0.0)
+        s = jnp.sum(total, axis=1, keepdims=True)
+        t = jnp.sum(picked, axis=1, keepdims=True)
+        st = jnp.where(lane == 0, m, jnp.where(lane == 1, s, jnp.where(lane == 2, t, 0.0))).T
+        for q in range(3):
+            sy[slot, q, pl.ds(k, 1)] = st[q:q + 1]
+
+    def running_sum(i):
+        at = rws(i * R, R)
+        carry = jnp.zeros((R, 1), jnp.float32)
+        for b in range(cb // TRI):
+            e = z_buf[at, b * TRI:(b + 1) * TRI]
             e1 = e.astype(jnp.bfloat16)
             r1 = e - e1.astype(jnp.float32)
             e2 = r1.astype(jnp.bfloat16)
@@ -205,42 +218,18 @@
                  + jnp.dot(e1, tri, preferred_element_type=jnp.float32)) + carry
             z_buf[at, b * TRI:(b + 1) * TRI] = c
             carry = c[:, TRI - 1:TRI]
-        t = jnp.sum(picked, axis=1, keepdims=True)
-        st = jnp.where(lane == 0, m, jnp.where(lane == 1, carry, jnp.where(lane == 2, t, 0.0))).T
-        for q in range(3):
-            sy[slot, q, pl.ds(k, 1)] = st[q:q + 1]
-
-    def sty(j):
-        return rdma(sy_a.at[me], sy_a.at[me], sty_ss.at[j - 1], sty_rs.at[me],
-                    {"hid": lax.rem(me + j, nh)})
+
+    na = nr - NB
 
     def stx(j):
         return rdma(sx_a.at[vi], sx_a.at[vi], stx_ss.at[j - 1], stx_rs.at[vi],
                     {"vocab": lax.rem(vi + j, nv)})
 
-    def merge_y():
-        for j in range(1, nh):
-            s = lax.rem(me + j, nh)
-            rdma(sy_a.at[s], sy_a.at[s], sty_ss.at[j - 1], sty_rs.at[s], to_up).wait_recv()
-        m_g = sy_a[0, 0]
-        for j in range(1, nh):
-            m_g = jnp.maximum(m_g, sy_a[j, 0])
-        zero = jnp.zeros_like(m_g)
-        s_g, t_g, pre = zero, zero, zero
-        for j in range(nh):
-            f = jnp.exp(sy_a[j, 0] - m_g)
-            s_j = sy_a[j, 1] * f
-            pre = pre + jnp.where(j < me, s_j, 0.0)
-            s_g = s_g + s_j
-            t_g = t_g + sy_a[j, 2] * f
-        sx_a[vi, 0] = m_g
-        sx_a[vi, 1] = s_g
-        sx_a[vi, 2] = t_g
-        for j in range(1, nv):
-            stx(j).start()
-        return m_g, pre
-
-    def merge_x(m_g, pre):
+    def sty(j):
+        return rdma(sy_out.at[j - 1], sy_a.at[me], sty_ss.at[j - 1], sty_rs.at[me],
+                    {"hid": lax.rem(me + j, nh)})
+
+    def merge_x():
         for j in range(1, nv):
             s = lax.rem(vi + j, nv)
             rdma(sx_a.at[s], sx_a.at[s], stx_ss.at[j - 1], stx_rs.at[s], to_nxt).wait_recv()
@@ -248,17 +237,41 @@
         for j in range(1, nv):
             big = jnp.maximum(big, sx_a[j, 0])
         zero = jnp.zeros_like(big)
-        tot, low, hit = zero, zero, zero
+        tot, low, hit, own_s = zero, zero, zero, zero
         for j in range(nv):
             f = jnp.exp(sx_a[j, 0] - big)
             s_j = sx_a[j, 1] * f
             low = low + jnp.where(j < vi, s_j, 0.0)
+            own_s = own_s + jnp.where(j == vi, s_j, 0.0)
             tot = tot + s_j
             hit = hit + sx_a[j, 2] * f
-        scale = jnp.exp(sy_a[me, 0] - big) / tot
-        off = (low + pre * jnp.exp(m_g - big)) / tot
-        hit_ref[...] = hit / tot
-        for i in range(last):
+        for q, v in enumerate((big, tot, hit, low)):
+            sy_a[me, q] = v
+        for j in range(1, nh):
+            below = low + jnp.where(me < lax.rem(me + j, nh), own_s, 0.0)
+            for q, v in enumerate((big, tot, hit, below)):
+                sy_out[j - 1, q] = v
+        for j in range(1, nh):
+            sty(j).start()
+
+    def merge_y():
+        for j in range(1, nh):
+            s = lax.rem(me + j, nh)
+            rdma(sy_out.at[j - 1], sy_a.at[s], sty_ss.at[j - 1], sty_rs.at[s], to_up).wait_recv()
+        big = sy_a[0, 0]
+        for j in range(1, nh):
+            big = jnp.maximum(big, sy_a[j, 0])
+        zero = jnp.zeros_like(big)
+        tot, low, hit = zero, zero, zero
+        for j in range(nh):
+            f = jnp.exp(sy_a[j, 0] - big)
+            tot = tot + sy_a[j, 1] * f
+            hit = hit + sy_a[j, 2] * f
+            low = low + sy_a[j, 3] * f
+        scale = jnp.exp(sx_a[vi, 0] - big) / tot
+        off = low / tot
+        hit_ref[0:na] = hit / tot
+        for i in range(na):
             finish(i * R, scale[i:i + 1], off[i:i + 1])
 
     nd = nv * nh
@@ -298,23 +311,32 @@
             low = low + jnp.where(j < own_slot, s_j, 0.0)
             tot = tot + s_j
             hit = hit + s_all[j, 2] * f
-        hit_ref[last:nr] = hit / tot
-        finish(last * R, jnp.exp(s_all[own_slot, 0] - big) / tot, low / tot)
-
-    last = nr - 1
-    for q in range(3):
-        sy_a[me, q, last:nr] = jnp.zeros((1, R), jnp.float32)
+        hit_ref[na:nr] = hit / tot
+        scale = jnp.exp(s_all[own_slot, 0] - big) / tot
+        off = low / tot
+        for i in range(NB):
+            finish((na + i) * R, scale[i:i + 1], off[i:i + 1])
 
     def block(i, _):
-        softmax(i, sy_a, me, i)
-        return 0
-
-    lax.fori_loop(0, last, block, 0)
-    for j in range(1, nh):
-        sty(j).start()
-    softmax(last, s_all, own_slot, 0)
-    lax.fori_loop(1, nd, send_all, 0)
-    got = merge_y()
+        softmax(i, sx_a, vi, i)
+        running_sum(i)
+        return 0
+
+    lax.fori_loop(0, na, block, 0)
+    for j in range(1, nv):
+        stx(j).start()
+
+    def late_block(i, _):
+        softmax(na + i, s_all, own_slot, i)
+        running_sum(na + i)
+        return 0
+
+    lax.fori_loop(0, NB - 1, late_block, 0)
+    merge_x()
+    softmax(nr - 1, s_all, own_slot, NB - 1)
+    for k in range(1, nd):
+        send_all(k, 0)
+    running_sum(nr - 1)
 
     for c in hy + leaf + direct + started:
         c.wait_send()
@@ -325,7 +347,7 @@
         return 0
 
     lax.fori_loop(0, nr, drain, 0)
-    merge_x(*got)
+    merge_y()
     lax.fori_loop(1, nd, hear_all, 0)
     merge_all()
     for j in range(1, nh):
@@ -380,9 +402,10 @@
                 pltpu.VMEM((2, rows, hc), f32),
                 pltpu.VMEM((nr, R), f32),
                 pltpu.VMEM((nr, R), jnp.int32),
-                pltpu.VMEM((nh, 3, nr, R), f32),
-                pltpu.VMEM((nv, 3, nr, R), f32),
-                pltpu.VMEM((nh * nv, 3, 1, R), f32),
+                pltpu.VMEM((nv, 3, nr - NB, R), f32),
+                pltpu.VMEM((nh - 1, 4, nr - NB, R), f32),
+                pltpu.VMEM((nh, 4, nr - NB, R), f32),
+                pltpu.VMEM((nh * nv, 3, NB, R), f32),
                 dma((6,)), dma((2,)), dma((2,)), dma((2, 8)), dma((2, 8)),
                 dma((2,)), dma((2,)), dma((2,)), dma((2,)),
                 dma((2, nr)), dma((2, nr)),

time: 142 us -> 141 us (level)
  no operation moved by 1% of the time
where the time goes in v4:
time: 141 us
  Pallas kernels  140 us (99%)
    pallas_call x1, Pallas kernels, local_step(): pl.pallas_call(functools.partial(head_kernel, nh, nv), name='head', out_s...  138 us

profile of v4, /device:TPU:97, one launch (start us, length us, event | category | flops | bytes accessed | tf_op | source)
XLA Modules:
  0.0 140.5 jit_solution(14815688848705007871)
XLA Ops:
  0.6 137.9 %head.1 = (f32[1024,1024]{1,0:T(8,128)S(1)}, f32[8,128]{1,0:T(8,128)S(1)}) custom-call(bf16[1024,1536]{1,0:T(8,128)(2,1)} %h_hbm.1, bf16[1536,4096]{1,0:T(8,128)(2,1)} %w_hbm.1, f32[8,128]{1,0:T(8,128)} %bitcast.3, s32[8,128]{1,0:T(8,128)} %bitcast.4), custom_call_target="tpu_custom_call" | custom-call | flops 12884901888 | bytes 19922944 | tf_op jit(solution)/shard_map/head/pallas_call | solution.py:388
  138.5 2.0 %store.1 = (f32[1024,1024]{1,0:T(8,128)}, f32[8,128]{1,0:T(8,128)}) custom-call(f32[1024,1024]{1,0:T(8,128)S(1)} %get-tuple-element.6.c_ref, f32[8,128]{1,0:T(8,128)S(1)} %get-tuple-element.7.hit_ref), custom_call_target="tpu_custom_call" | custom-call | tf_op jit(solution)/shard_map/store/pallas_call | solution.py:421

commit v5 on v4

--- a/solution.py
+++ b/solution.py
@@ -12,13 +12,14 @@
 LANES = 128
 NC = 1
 NB = 2
+PARTS = ((0, 64), (64, 32), (96, 32))
 TRI = 256
 
 
 def head_kernel(nh, nv, h_hbm, w_hbm, temp_hbm, tgt_hbm,
                 z_buf, hit_ref,
                 h_own, h_nb, w_sum, w_own, w_leaf, w_dir, s_send, s_recv, temp_ref, tgt_ref,
-                sx_a, sy_out, sy_a, s_all,
+                sx_a, sy_out, sy_a, s_all, st_buf,
                 ld_sem, hy_ss, hy_rs, hx_ss, hx_rs, leaf_ss, leaf_rs, dir_ss, dir_rs,
                 sum_ss, sum_rs, sty_ss, sty_rs, stx_ss, stx_rs, all_ss, all_rs):
     rows, depth = h_hbm.shape
@@ -138,21 +139,36 @@
     for c in leaf:
         c.wait_recv()
 
+    last = nr - 1
+
+    def sum_part(p, start, n, k):
+        at = rws(start, n)
+        return rdma(s_send.at[p, at], s_recv.at[p, at], sum_ss.at[p, k], sum_rs.at[p, k],
+                    to_dn if p == 0 else to_up)
+
     def sum_copy(p, i):
-        at = rws(i * R, R)
-        return rdma(s_send.at[p, at], s_recv.at[p, at], sum_ss.at[p, i], sum_rs.at[p, i],
-                    to_dn if p == 0 else to_up)
-
-    def add_leaf(i, _):
+        return sum_part(p, i * R, R, i)
+
+    last_sums = [[sum_part(p, last * R + lo, n, last + k) for p in range(2)]
+                 for k, (lo, n) in enumerate(PARTS)]
+
+    def add_leaf(i):
         at = rws(i * R, R)
         for p in range(2):
             s_send[p, at] = s_send[p, at] + jnp.dot(
                 h_nb[p, at], w_leaf[p], preferred_element_type=jnp.float32)
+
+    def sums(i, _):
+        add_leaf(i)
         for p in range(2):
             sum_copy(p, i).start()
         return 0
 
-    lax.fori_loop(0, nr, add_leaf, 0)
+    lax.fori_loop(0, last, sums, 0)
+    add_leaf(last)
+    for pair in last_sums:
+        for c in pair:
+            c.start()
 
     for c in direct:
         c.wait_recv()
@@ -172,17 +188,22 @@
             sl = slice(j * LANES, (j + 1) * LANES)
             z_buf[start:start + R, sl] = z_buf[start:start + R, sl] * a + b
 
-    def softmax(i, sy, slot, k):
+    def row_values(i):
+        temp = jnp.concatenate([by_row(temp_ref[pl.ds(i, 1)])] * (TRI // LANES), axis=1)
+        tgt = jnp.concatenate(
+            [by_row(tgt_ref[pl.ds(i, 1)].astype(jnp.float32) - first_tok)] * (TRI // LANES), axis=1)
+        return temp, tgt
+
+    def add_direct(i):
         at = rws(i * R, R)
         for p in range(2):
             sl = slice(p * hc, (p + 1) * hc)
             z_buf[at, sl] = z_buf[at, sl] + jnp.dot(
                 h_nb[1 - p, at], w_dir[p], preferred_element_type=jnp.float32)
-        temp = jnp.concatenate([by_row(temp_ref[pl.ds(i, 1)])] * (TRI // LANES), axis=1)
-        tgt = jnp.concatenate(
-            [by_row(tgt_ref[pl.ds(i, 1)].astype(jnp.float32) - first_tok)] * (TRI // LANES), axis=1)
-        for p in range(2):
-            sum_copy(p, i).wait_recv()
+
+    def exps(start, lo, n, temp, tgt):
+        at = rws(start, n)
+        temp, tgt = temp[lo:lo + n], tgt[lo:lo + n]
         m = None
         zs = []
         for b in range(cb // TRI):
@@ -191,18 +212,39 @@
             zs.append(z)
             m = z if m is None else jnp.maximum(m, z)
         m = jnp.max(m, axis=1, keepdims=True)
-        total = jnp.zeros((R, TRI), jnp.float32)
-        picked = jnp.zeros((R, TRI), jnp.float32)
+        total = jnp.zeros((n, TRI), jnp.float32)
+        picked = jnp.zeros((n, TRI), jnp.float32)
         for b in range(cb // TRI):
             e = jnp.exp(zs[b] - m)
             z_buf[at, b * TRI:(b + 1) * TRI] = e
             total = total + e
-            picked = picked + jnp.where(col + float(b * TRI) <= tgt, e, 0.0)
+            picked = picked + jnp.where(col[:n] + float(b * TRI) <= tgt, e, 0.0)
         s = jnp.sum(total, axis=1, keepdims=True)
         t = jnp.sum(picked, axis=1, keepdims=True)
-        st = jnp.where(lane == 0, m, jnp.where(lane == 1, s, jnp.where(lane == 2, t, 0.0))).T
+        ln = lane[:n]
+        st_buf[lo:lo + n] = jnp.where(ln == 0, m, jnp.where(ln == 1, s, jnp.where(ln == 2, t, 0.0)))
+
+    def publish(sy, slot, k):
+        st = st_buf[...].T
         for q in range(3):
             sy[slot, q, pl.ds(k, 1)] = st[q:q + 1]
+
+    def softmax(i, sy, slot, k):
+        add_direct(i)
+        temp, tgt = row_values(i)
+        for p in range(2):
+            sum_copy(p, i).wait_recv()
+        exps(i * R, 0, R, temp, tgt)
+        publish(sy, slot, k)
+
+    def softmax_last(sy, slot, k):
+        add_direct(last)
+        temp, tgt = row_values(last)
+        for (lo, n), pair in zip(PARTS, last_sums):
+            for c in pair:
+                c.wait_recv()
+            exps(last * R + lo, lo, n, temp, tgt)
+        publish(sy, slot, k)
 
     def running_sum(i):
         at = rws(i * R, R)
@@ -277,27 +319,24 @@
     nd = nv * nh
     own_slot = vi * nh + me
 
+    def hops(k):
+        v, h = k // nh, k % nh
+        return min((v + 1) // 2, (nv - v + 1) // 2) + min(h, nh - h)
+
+    near_first = sorted(range(1, nd), key=hops)
+
     def peer(k):
-        return lax.rem(vi + k // nh, nv), lax.rem(me + lax.rem(k, nh), nh)
+        return lax.rem(vi + k // nh, nv), lax.rem(me + k % nh, nh)
 
     def sta(k):
         v, h = peer(k)
         return rdma(s_all.at[own_slot], s_all.at[own_slot], all_ss.at[k], all_rs.at[own_slot],
                     {"hid": h, "vocab": v})
 
-    def send_all(k, _):
-        sta(k).start()
-        return 0
-
-    def hear_all(k, _):
+    def hear(k):
         v, h = peer(k)
         s = v * nh + h
         rdma(s_all.at[s], s_all.at[s], all_ss.at[k], all_rs.at[s], to_up).wait_recv()
-        return 0
-
-    def sent_all(k, _):
-        sta(k).wait_send()
-        return 0
 
     def merge_all():
         big = s_all[0, 0]
@@ -333,10 +372,10 @@
 
     lax.fori_loop(0, NB - 1, late_block, 0)
     merge_x()
-    softmax(nr - 1, s_all, own_slot, NB - 1)
-    for k in range(1, nd):
-        send_all(k, 0)
-    running_sum(nr - 1)
+    softmax_last(s_all, own_slot, NB - 1)
+    for k in reversed(near_first):
+        sta(k).start()
+    running_sum(last)
 
     for c in hy + leaf + direct + started:
         c.wait_send()
@@ -346,15 +385,20 @@
             sum_copy(p, i).wait_send()
         return 0
 
-    lax.fori_loop(0, nr, drain, 0)
+    lax.fori_loop(0, last, drain, 0)
+    for pair in last_sums:
+        for c in pair:
+            c.wait_send()
+    for j in range(1, nv):
+        stx(j).wait_send()
     merge_y()
-    lax.fori_loop(1, nd, hear_all, 0)
-    merge_all()
     for j in range(1, nh):
         sty(j).wait_send()
-    for j in range(1, nv):
-        stx(j).wait_send()
-    lax.fori_loop(1, nd, sent_all, 0)
+    for k in near_first:
+        sta(k).wait_send()
+    for k in near_first:
+        hear(k)
+    merge_all()
 
 
 def store_kernel(nc, c_ref, hit_ref, out_hbm, hit_hbm, sem):
@@ -406,9 +450,10 @@
                 pltpu.VMEM((nh - 1, 4, nr - NB, R), f32),
                 pltpu.VMEM((nh, 4, nr - NB, R), f32),
                 pltpu.VMEM((nh * nv, 3, NB, R), f32),
+                pltpu.VMEM((R, LANES), f32),
                 dma((6,)), dma((2,)), dma((2,)), dma((2, 8)), dma((2, 8)),
                 dma((2,)), dma((2,)), dma((2,)), dma((2,)),
-                dma((2, nr)), dma((2, nr)),
+                dma((2, nr - 1 + len(PARTS))), dma((2, nr - 1 + len(PARTS))),
                 dma((nh - 1,)), dma((nh,)), dma((nv - 1,)), dma((nv,)), dma((nh * nv,)), dma((nh * nv,)),
             ],
             cost_estimate=pl.CostEstimate(

time: 141 us -> 140 us (level)
  no operation moved by 1% of the time
where the time goes in v5:
time: 140 us
  Pallas kernels  139 us (99%)
    pallas_call x1, Pallas kernels, local_step(): pl.pallas_call(functools.partial(head_kernel, nh, nv), name='head', out_s...  137 us

profile of v5, /device:TPU:97, one launch (start us, length us, event | category | flops | bytes accessed | tf_op | source)
XLA Modules:
  0.0 139.7 jit_solution(1279588585594744220)
XLA Ops:
  0.6 137.1 %head.1 = (f32[1024,1024]{1,0:T(8,128)S(1)}, f32[8,128]{1,0:T(8,128)S(1)}) custom-call(bf16[1024,1536]{1,0:T(8,128)(2,1)} %h_hbm.1, bf16[1536,4096]{1,0:T(8,128)(2,1)} %w_hbm.1, f32[8,128]{1,0:T(8,128)} %bitcast.3, s32[8,128]{1,0:T(8,128)} %bitcast.4), custom_call_target="tpu_custom_call" | custom-call | flops 12884901888 | bytes 19922944 | tf_op jit(solution)/shard_map/head/pallas_call | solution.py:432
  137.7 2.0 %store.1 = (f32[1024,1024]{1,0:T(8,128)}, f32[8,128]{1,0:T(8,128)}) custom-call(f32[1024,1024]{1,0:T(8,128)S(1)} %get-tuple-element.6.c_ref, f32[8,128]{1,0:T(8,128)S(1)} %get-tuple-element.7.hit_ref), custom_call_target="tpu_custom_call" | custom-call | tf_op jit(solution)/shard_map/store/pallas_call | solution.py:466
